TPU v7x, 32 devices: a whole 2x2x4 slice. The times are simulated.
32 devices in a mesh: dp: 16 (over z, y, core), mp: 2 (over x).
Axes of the slice: x: 2, y: 2, z: 4, core: 2. Of those that a mesh axis runs over, the one named last changes fastest.
Arguments:
- inputs: bfloat16 [4, 4096, 4096], P(None, 'dp'), may hold values from -60 to 60
- gate_cotangent: bfloat16 [4, 4096, 6144], P(None, 'dp', 'mp'), may hold values from -6 to 6
- ff_blocks: int32 [4], replicated, may hold values from 24 to 48, as said below
- layer_active: int32 [4], replicated, may hold values from 0 to 1, as said below
- param: float32 [4096, 6144], P(('dp', 'mp')), may hold values from -0.09375 to 0.09375
- moment: float32 [4096, 6144], P(('dp', 'mp')), may hold values from -3 to 3
- second_moment: float32 [4096, 6144], P(('dp', 'mp')), may hold values from 0.5 to 2
Outputs:
- new_param: float32 [4096, 6144], P(('dp', 'mp'))
- new_moment: float32 [4096, 6144], P(('dp', 'mp'))
- new_second: float32 [4096, 6144], P(('dp', 'mp'))
Inputs may be any that keep to these rules, and one draw needn't show every extreme that they name: `ff_blocks`: entry 0 is 6144 // 128 (the largest subnet), entry 1 is 6144 // (256) (the smallest). `layer_active`: entry 0 is 1, and exactly one of entries 1, 2 and 3 is 0.
All inputs are finite; a program needn't handle non-finite values.
Results may differ from a plain program's by a relative error of at most 0.0003.
Values sent between devices are 32-bit elements; how exact they have to be, the bound alone decides.
A program may use at most 128 MiB of HBM per device.

v0:
```python
import functools
import math

import jax
import jax.numpy as jnp
from jax import lax
from jax.experimental import pallas as pl
from jax.experimental.pallas import tpu as pltpu
from jax.sharding import PartitionSpec as P

BLOCK = 128
STEP = 10
MESH = pl.DeviceIdType.MESH
RING = 6


class Plan:
    def __init__(self, replicas, owners, width, local_cols, tokens):
        self.replicas, self.owners, self.tokens = replicas, owners, tokens
        self.line = line = replicas // 4
        self.rows = width // replicas
        self.part = self.rows // owners
        self.width, self.cols = width, local_cols
        self.wide = wide = 256 if local_cols % 512 == 0 else 128
        self.chunks = chunks = local_cols // wide
        self.half = half = chunks // 2
        self.crossings = line * chunks - half
        self.lag = 0
        while not self.fits():
            self.lag += 1
            assert self.lag < 1000
        self.ticks = self.last + chunks

    def fits(self):
        line, chunks, half = self.line, self.chunks, self.half
        self.last = (line - 1) * chunks - half + 4 + self.lag
        self.order = []
        good = True
        for at in range(line // 2):
            need = []
            for k in range(line):
                for h in range(2):
                    if (k, h) != (at ^ 1, 0):
                        need.append((self.tick_of(at, k, h * half), k, h))
            self.order.append([(k, h) for _, k, h in sorted(need)])
            for p, (k, h) in enumerate(self.order[-1]):
                for i in range(half):
                    good &= p * half + i <= self.tick_of(at, k, h * half + i)
                    good &= k != at or h == 1 or p * half + i > i
            good &= at == 0 or self.tick_of(at, at + 1, chunks - 1) < self.last
            good &= at == 0 or self.tick_of(at, at - 1, chunks - 1) < self.last
        return good

    def start(self, distance):
        return self.lag + (self.half + 2 + 2 * distance if distance else 4)

    def tick_of(self, at, k, j):
        if k == at:
            return self.last + j
        if k > at:
            return self.start(at) + (self.line - 1 - k) * self.chunks + j
        return self.start(self.line - 1 - at) + k * self.chunks + j


def pick(table, at, p):
    value = jnp.int32(0)
    for a, row in enumerate(table):
        for q, entry in enumerate(row):
            if entry:
                value = jnp.where((at == a) & (p == q), jnp.int32(entry), value)
    return value


def kernel(plan, ff, active, x_hbm, c_hbm, g_hbm, total_ref, x, c, xt, w, yr, z, dr, ds, sb, rb, ob, g, sq, parts,
           load_sem, d2d_send, d2d_recv, y_send, y_recv, z_send, z_recv, d_send, d_recv, x_send, x_recv, out_sem,
           p_send, p_recv):
    line, chunks, half, rows, wide = plan.line, plan.chunks, plan.half, plan.rows, plan.wide
    owners, part = plan.owners, plan.part
    dp, mp = lax.axis_index("dp"), lax.axis_index("mp")
    devices = plan.replicas * owners
    me = dp * owners + mp
    place, lane, core = dp // 4, (dp // 2) % 2, dp % 2
    other_core, other_lane = dp + 1 - 2 * core, dp + 2 - 4 * lane
    beside = place + 1 - 2 * (place % 2)
    far = place >= line // 2
    at = jnp.where(far, line - 1 - place, place)

    def mirrored(k):
        return jnp.where(far, line - 1 - k, k)

    loads = [
        pltpu.make_async_copy(c_hbm, c, load_sem.at[0]),
        pltpu.make_async_copy(x_hbm, x, load_sem.at[1]),
    ]
    for load in loads:
        load.start()
    barrier = pltpu.get_barrier_semaphore()

    @pl.loop(1, devices)
    def _(o):
        other = lax.rem(me + o, devices)
        pl.semaphore_signal(barrier, inc=1, device_id=(other // owners, other % owners), device_id_type=MESH)

    loads[0].wait()
    first_block = mp * (plan.cols // BLOCK)
    subnets = ff.shape[0]
    tokens = plan.tokens // subnets

    @pl.loop(0, plan.cols // BLOCK)
    def _(b):
        cols = pl.ds(pl.multiple_of(b * BLOCK, BLOCK), BLOCK)
        for s in range(subnets):
            keep = (first_block + b < ff[s]) & (active[s] == 1)
            spot = (pl.ds(s * tokens, tokens), cols)
            c[spot] = jnp.where(keep, c[spot], jnp.zeros((), c.dtype))

    sq[...] = jnp.zeros_like(sq)
    loads[1].wait()
    pl.semaphore_wait(barrier, devices - 1)

    def core_copy(q, parity):
        return pltpu.make_async_remote_copy(
            sb.at[q], rb.at[parity, q], d2d_send.at[q], d2d_recv.at[parity, q], device_id=(other_core, mp), device_id_type=MESH
        )

    def y_copy(slot, idx):
        return pltpu.make_async_remote_copy(
            w.at[slot], yr.at[idx], y_send.at[slot], y_recv.at[idx], device_id=(other_lane, mp), device_id_type=MESH
        )

    def d_copy(j):
        return pltpu.make_async_remote_copy(
            ds.at[j], dr.at[j], d_send.at[j], d_recv.at[j], device_id=(dp + 4 * (beside - place), mp), device_id_type=MESH
        )

    def z_copy(idx, slot, to):
        return pltpu.make_async_remote_copy(
            yr.at[idx], z.at[slot], z_send.at[idx], z_recv.at[slot], device_id=(dp + 4 * (to - place), mp), device_id_type=MESH
        )

    def x_copy(o, j):
        to = lax.rem(mp + o, owners)
        spot = yr.at[place * chunks + j, pl.ds(pl.multiple_of(to * part, part), part)]
        return pltpu.make_async_remote_copy(
            spot, g.at[mp * chunks + j], x_send.at[(o - 1) * chunks + j], x_recv.at[mp * chunks + j],
            device_id=(dp, to), device_id_type=MESH,
        )

    def part_copy(o):
        other = lax.rem(me + o, devices)
        return pltpu.make_async_remote_copy(
            parts.at[0], parts.at[devices - o], p_send, p_recv, device_id=(other // owners, other % owners), device_id_type=MESH
        )

    def out_copy(i):
        return pltpu.make_async_copy(
            g.at[i], g_hbm.at[:, pl.ds(pl.multiple_of(i * wide, wide), wide)], out_sem.at[i]
        )

    def produce(q, on, k, to_lane, j, fresh, parity):
        @pl.when(on)
        def _():
            @pl.when(fresh)
            def _():
                for side, owner in enumerate((1 - core, core)):
                    first = pl.multiple_of(((k * 2 + to_lane) * 2 + owner) * rows, rows)
                    xt[q, side] = x[:, pl.ds(first, rows)].T

            cols = pl.ds(pl.multiple_of(j * wide, wide), wide)
            sb[q] = jnp.dot(xt[q, 0], c[:, cols], preferred_element_type=jnp.float32)
            ob[q] = jnp.dot(xt[q, 1], c[:, cols], preferred_element_type=jnp.float32)
            core_copy(q, parity).start()

    def own(q, on, k, j, parity):
        idx = k * chunks + j

        @pl.when(on)
        def _():
            core_copy(q, parity).wait()
            crossed = (k != beside) | (j >= half)

            @pl.when(crossed)
            def _():
                y_copy(0, idx).wait_recv()
                yr[idx] = yr[idx] + (ob[q] + rb[parity, q])

            @pl.when(jnp.logical_not(crossed))
            def _():
                yr[idx] = ob[q] + rb[parity, q]

            @pl.when((k >= place) & (place > 0))
            def _():
                z_copy(idx, idx, place).wait_recv()
                yr[idx] = yr[idx] + z[idx]

            @pl.when((k <= place) & (place < line - 1))
            def _():
                slot = jnp.where(k == place, line, k) * chunks + j
                z_copy(idx, slot, place).wait_recv()
                yr[idx] = yr[idx] + z[slot]

            @pl.when(k != place)
            def _():
                to = jnp.where(k > place, place + 1, place - 1)
                slot = jnp.where(k == place - 1, line, k) * chunks + j
                z_copy(idx, slot, to).start()

            @pl.when(k == place)
            def _():
                for o in range(1, owners):
                    x_copy(o, j).start()
                value = yr[idx]
                sq[...] += jnp.sum((value * value).reshape(rows // 8, 8, wide), axis=0)
                g[mp * chunks + j] = yr[idx, pl.ds(pl.multiple_of(mp * part, part), part)]

    @pl.loop(0, plan.ticks)
    def _(t):
        parity = lax.rem(t, 2)
        phase, step = t // half, lax.rem(t, half)
        crossing = t < plan.crossings
        y_k = mirrored(pick([[k for k, _ in row] for row in plan.order], at, phase))
        y_j = pick([[h for _, h in row] for row in plan.order], at, phase) * half + step
        deferring = t < half
        ahead = plan.lag + jnp.where(at == 0, 4, half + 2 + 2 * at)
        i = t - ahead
        forward = (i >= 0) & (i < (line - 1 - at) * chunks)
        ending = (t >= plan.last)
        i = jnp.maximum(i, 0)
        m_on = forward | (ending & (at > 0))
        m_k = mirrored(jnp.where(forward, line - 1 - i // chunks, at))
        m_j = jnp.where(forward, i % chunks, t - plan.last)
        n = t - (plan.lag + half + 2 + 2 * (line - 1 - at))
        backward = (at > 0) & (n >= 0) & (n < at * chunks)
        n = jnp.maximum(n, 0)
        s_on = backward | (ending & (at == 0))
        s_k = mirrored(jnp.where(backward, n // chunks, at))
        s_j = jnp.where(backward, n % chunks, t - plan.last)

        produce(0, crossing, y_k, 1 - lane, y_j, step == 0, parity)
        produce(1, deferring, beside, 1 - lane, t, t == 0, parity)
        produce(2, m_on, m_k, lane, m_j, m_j == 0, parity)
        produce(3, s_on, s_k, lane, s_j, s_j == 0, parity)

        slot = lax.rem(t, RING)
        y_idx = y_k * chunks + y_j

        @pl.when(crossing)
        def _():
            @pl.when(t >= RING)
            def _():
                y_copy(slot, 0).wait_send()

            core_copy(0, parity).wait()
            w[slot] = ob[0] + rb[parity, 0]

            @pl.when((y_k == place) & (y_j < half))
            def _():
                d_copy(y_j).wait_recv()
                w[slot] = w[slot] + dr[y_j]

            y_copy(slot, y_idx).start()

        @pl.when(deferring)
        def _():
            core_copy(1, parity).wait()
            ds[t] = ob[1] + rb[parity, 1]
            d_copy(t).start()

        own(2, m_on, m_k, m_j, parity)
        own(3, s_on, s_k, s_j, parity)

    total = sq[:, pl.ds(0, 128)]
    for i in range(1, wide // 128):
        total = total + sq[:, pl.ds(i * 128, 128)]
    parts[0] = total

    @pl.loop(1, devices)
    def _(o):
        part_copy(o).start()

    @pl.loop(0, chunks)
    def _(j):
        out_copy(mp * chunks + j).start()

    for o in range(1, owners):
        @pl.loop(0, chunks)
        def _(j):
            i = lax.rem(mp + o, owners) * chunks + j
            pltpu.make_async_remote_copy(
                g.at[i], g.at[i], x_send.at[0], x_recv.at[i], device_id=(dp, mp), device_id_type=MESH
            ).wait_recv()
            out_copy(i).start()

    others = parts.at[pl.ds(1, devices - 1)]
    everyone = pltpu.make_async_remote_copy(others, others, p_send, p_recv, device_id=(dp, mp), device_id_type=MESH)
    everyone.wait_recv()
    total_ref[...] = jnp.full(total_ref.shape, jnp.sum(jnp.sum(parts[...], axis=0)))
    everyone.wait_send()

    @pl.loop(0, owners * chunks)
    def _(i):
        out_copy(i).wait()

    @pl.loop(0, half)
    def _(j):
        d_copy(j).wait_send()

    @pl.loop(0, RING)
    def _(slot):
        y_copy(slot, 0).wait_send()

    @pl.loop(0, line * chunks)
    def _(i):
        @pl.when(i // chunks != place)
        def _():
            z_copy(i, 0, place).wait_send()

    for o in range(1, owners):
        @pl.loop(0, chunks)
        def _(j):
            x_copy(o, j).wait_send()


def reduced_gradient(plan, ff_blocks, layer_active, rows_in, rows_ct):
    rows, wide, chunks, line, half = plan.rows, plan.wide, plan.chunks, plan.line, plan.half
    devices = plan.replicas * plan.owners
    f32, dma = jnp.float32, pltpu.SemaphoreType.DMA

    def held(*lead):
        return pltpu.VMEM((*lead, rows, wide), f32)

    return pl.pallas_call(
        functools.partial(kernel, plan),
        out_shape=(
            jax.ShapeDtypeStruct((plan.part, plan.owners * plan.cols), f32),
            jax.ShapeDtypeStruct((8, 128), f32),
        ),
        in_specs=[
            pl.BlockSpec(memory_space=pltpu.SMEM),
            pl.BlockSpec(memory_space=pltpu.SMEM),
            pl.BlockSpec(memory_space=pl.ANY),
            pl.BlockSpec(memory_space=pl.ANY),
        ],
        out_specs=(pl.BlockSpec(memory_space=pl.ANY), pl.BlockSpec(memory_space=pltpu.VMEM)),
        scratch_shapes=[
            pltpu.VMEM((plan.tokens, plan.width), jnp.bfloat16),
            pltpu.VMEM((plan.tokens, plan.cols), jnp.bfloat16),
            pltpu.VMEM((4, 2, rows, plan.tokens), jnp.bfloat16),
            held(RING),
            held(line * chunks),
            held((line + 1) * chunks),
            held(half),
            held(half),
            held(4),
            held(2, 4),
            held(4),
            pltpu.VMEM((plan.owners * chunks, plan.part, wide), f32),
            pltpu.VMEM((8, wide), f32),
            pltpu.VMEM((devices, 8, 128), f32),
            dma((2,)),
            dma((4,)),
            dma((2, 4)),
            dma((RING,)),
            dma((line * chunks,)),
            dma((line * chunks,)),
            dma(((line + 1) * chunks,)),
            dma((half,)),
            dma((half,)),
            dma((max(1, plan.owners - 1) * chunks,)),
            dma((plan.owners * chunks,)),
            dma((plan.owners * chunks,)),
            dma,
            dma,
        ],
        compiler_params=pltpu.CompilerParams(collective_id=0, has_side_effects=True, vmem_limit_bytes=67043328),
        cost_estimate=pl.CostEstimate(
            flops=2 * plan.tokens * plan.width * plan.cols, bytes_accessed=32 << 20, transcendentals=0
        ),
        name="reduced_gradient",
    )(ff_blocks, layer_active, rows_in, rows_ct)


def shards(inputs, gate_cotangent, ff_blocks, layer_active, param, moment, second_moment):
    subnets, tokens, width = inputs.shape
    local_cols = gate_cotangent.shape[2]
    replicas, owners = lax.axis_size("dp"), lax.axis_size("mp")
    plan = Plan(replicas, owners, width, local_cols, subnets * tokens)
    gradient, total_sq = reduced_gradient(
        plan,
        ff_blocks,
        layer_active,
        inputs.reshape(subnets * tokens, width),
        gate_cotangent.reshape(subnets * tokens, local_cols),
    )
    total = jnp.sqrt(total_sq[0, 0])
    factor = jnp.minimum(1.0, math.sqrt(1.0 * width * local_cols * owners) / (total + 1e-06))
    clipped = gradient * factor
    new_moment = 0.9 * moment + 0.1 * clipped
    new_second = 0.95 * second_moment + 0.05 * clipped * clipped
    first_hat = new_moment / (1.0 - 0.9**STEP)
    second_hat = new_second / (1.0 - 0.95**STEP)
    new_param = param - 0.02 * (first_hat / (jnp.sqrt(second_hat) + 1e-08) + 0.1 * param)
    return (new_param, new_moment, new_second)


def solution(mesh):
    in_specs = (
        P(None, "dp", None),
        P(None, "dp", "mp"),
        P(),
        P(),
        P(("dp", "mp"), None),
        P(("dp", "mp"), None),
        P(("dp", "mp"), None),
    )
    out_specs = (P(("dp", "mp"), None), P(("dp", "mp"), None), P(("dp", "mp"), None))
    return jax.shard_map(shards, mesh=mesh, in_specs=in_specs, out_specs=out_specs, check_vma=False)
```

profile of v0, /device:TPU:0, one launch (start us, length us, event | category | flops | bytes accessed | tf_op | source)
XLA Modules:
  0.0 270.3 jit_solution(8868846561194158551)
XLA Ops:
  0.6 259.4 %reduced_gradient.1 = (f32[128,6144]{1,0:T(8,128)}, f32[8,128]{1,0:T(8,128)}) custom-call(s32[4]{0:T(128)} %ff.1, s32[4]{0:T(128)} %active.1, bf16[1024,4096]{1,0:T(8,128)(2,1)} %bitcast.3, bf16[1024,3072]{1,0:T(8,128)(2,1)} %bitcast.4), custom_call_target="tpu_custom_call" | custom-call | flops 25769803776 | bytes 33554432 | tf_op jit(solution)/shard_map/reduced_gradient/pallas_call | solution.py:332
  260.0 1.2 slice.3
  262.0 8.3 %multiply_subtract_fusion = (f32[128,6144]{1,0:T(8,128)}, f32[128,6144]{1,0:T(8,128)}, f32[128,6144]{1,0:T(8,128)}) fusion(f32[128,6144]{1,0:T(8,128)} %param.11, f32[128,6144]{1,0:T(8,128)} %get-tuple-element.5, f32[]{:T(128)} %bitcast.2, f32[128,6144]{1,0:T(8,128)} %param.12, f32[128,6144]{1,0:T(8,128)} %param.13), kind=kLoop, calls=%fused_computation.2 | loop fusion | flops 12582912 | bytes 22020100 | tf_op jit(solution)/shard_map/sub | solution.py:402
where the time goes:
time: 271 us; the launch traced here: 270 us
  Pallas kernels  259 us (96%)
  other arithmetic  8.31 us (3%)
    pallas_call x1, Pallas kernels, reduced_gradient(): pl.pallas_call(functools.partial(kernel, plan), out_shape=(jax.ShapeDtype...  259 us
    sub x1, other arithmetic, shards(): param - 0.02 * (first_hat / (jnp.sqrt(second_hat) + 1e-08) + 0.1 * param)  8.31 us

commit v1 on v0

--- a/solution.py
+++ b/solution.py
@@ -11,7 +11,7 @@
 BLOCK = 128
 STEP = 10
 MESH = pl.DeviceIdType.MESH
-RING = 6
+RING = 4
 
 
 class Plan:
@@ -47,6 +47,7 @@
                 for i in range(half):
                     good &= p * half + i <= self.tick_of(at, k, h * half + i)
                     good &= k != at or h == 1 or p * half + i > i
+            good &= self.order[-1][0][1] == 0
             good &= at == 0 or self.tick_of(at, at + 1, chunks - 1) < self.last
             good &= at == 0 or self.tick_of(at, at - 1, chunks - 1) < self.last
         return good
@@ -71,8 +72,8 @@
     return value
 
 
-def kernel(plan, ff, active, x_hbm, c_hbm, g_hbm, total_ref, x, c, xt, w, yr, z, dr, ds, sb, rb, ob, g, sq, parts,
-           load_sem, d2d_send, d2d_recv, y_send, y_recv, z_send, z_recv, d_send, d_recv, x_send, x_recv, out_sem,
+def kernel(plan, limit, x_hbm, c_hbm, g_hbm, total_ref, x, c, xt, w, yr, z, dr, sb, rb, ob, sq, parts,
+           x_load, c_load, d2d_send, d2d_recv, y_send, y_recv, z_send, z_recv, d_send, d_recv, x_send, x_recv, keep_sem,
            p_send, p_recv):
     line, chunks, half, rows, wide = plan.line, plan.chunks, plan.half, plan.rows, plan.wide
     owners, part = plan.owners, plan.part
@@ -88,12 +89,19 @@
     def mirrored(k):
         return jnp.where(far, line - 1 - k, k)
 
-    loads = [
-        pltpu.make_async_copy(c_hbm, c, load_sem.at[0]),
-        pltpu.make_async_copy(x_hbm, x, load_sem.at[1]),
-    ]
-    for load in loads:
-        load.start()
+    def x_in(k, to_lane):
+        block = k * 2 + to_lane
+        cols = pl.ds(pl.multiple_of(block * 2 * rows, 2 * rows), 2 * rows)
+        return pltpu.make_async_copy(x_hbm.at[:, cols], x.at[:, cols], x_load.at[block])
+
+    def c_in(j):
+        cols = pl.ds(pl.multiple_of(j * wide, wide), wide)
+        return pltpu.make_async_copy(c_hbm.at[:, cols], c.at[:, cols], c_load.at[j])
+
+    opening = mirrored(pick([[row[0][0]] for row in plan.order], at, 0))
+    x_in(opening, 1 - lane).start()
+    c_in(0).start()
+    x_in(beside, 1 - lane).start()
     barrier = pltpu.get_barrier_semaphore()
 
     @pl.loop(1, devices)
@@ -101,22 +109,34 @@
         other = lax.rem(me + o, devices)
         pl.semaphore_signal(barrier, inc=1, device_id=(other // owners, other % owners), device_id_type=MESH)
 
-    loads[0].wait()
+    def load_rest():
+        @pl.loop(1, chunks)
+        def _(j):
+            c_in(j).start()
+
+        @pl.loop(0, line)
+        def _(k):
+            @pl.when((k != opening) & (k != beside))
+            def _():
+                x_in(k, 1 - lane).start()
+
+            x_in(k, lane).start()
+
     first_block = mp * (plan.cols // BLOCK)
-    subnets = ff.shape[0]
+    subnets = limit.shape[0]
     tokens = plan.tokens // subnets
 
-    @pl.loop(0, plan.cols // BLOCK)
-    def _(b):
-        cols = pl.ds(pl.multiple_of(b * BLOCK, BLOCK), BLOCK)
-        for s in range(subnets):
-            keep = (first_block + b < ff[s]) & (active[s] == 1)
-            spot = (pl.ds(s * tokens, tokens), cols)
-            c[spot] = jnp.where(keep, c[spot], jnp.zeros((), c.dtype))
+    def ready(j):
+        c_in(j).wait()
+        for i in range(wide // BLOCK):
+            b = j * (wide // BLOCK) + i
+            cols = pl.ds(pl.multiple_of(b * BLOCK, BLOCK), BLOCK)
+            for s in range(subnets):
+                keep = first_block + b < limit[s]
+                spot = (pl.ds(s * tokens, tokens), cols)
+                c[spot] = jnp.where(keep, c[spot], jnp.zeros((), c.dtype))
 
     sq[...] = jnp.zeros_like(sq)
-    loads[1].wait()
-    pl.semaphore_wait(barrier, devices - 1)
 
     def core_copy(q, parity):
         return pltpu.make_async_remote_copy(
@@ -130,36 +150,43 @@
 
     def d_copy(j):
         return pltpu.make_async_remote_copy(
-            ds.at[j], dr.at[j], d_send.at[j], d_recv.at[j], device_id=(dp + 4 * (beside - place), mp), device_id_type=MESH
+            yr.at[beside * chunks + j], dr.at[j], d_send.at[j], d_recv.at[j], device_id=(dp + 4 * (beside - place), mp), device_id_type=MESH
         )
 
     def z_copy(idx, slot, to):
         return pltpu.make_async_remote_copy(
             yr.at[idx], z.at[slot], z_send.at[idx], z_recv.at[slot], device_id=(dp + 4 * (to - place), mp), device_id_type=MESH
         )
+
+    def result(i):
+        return g_hbm.at[:, pl.ds(pl.multiple_of(i * wide, wide), wide)]
 
     def x_copy(o, j):
         to = lax.rem(mp + o, owners)
         spot = yr.at[place * chunks + j, pl.ds(pl.multiple_of(to * part, part), part)]
         return pltpu.make_async_remote_copy(
-            spot, g.at[mp * chunks + j], x_send.at[(o - 1) * chunks + j], x_recv.at[mp * chunks + j],
+            spot, result(mp * chunks + j), x_send.at[(o - 1) * chunks + j], x_recv.at[mp * chunks + j],
             device_id=(dp, to), device_id_type=MESH,
         )
+
+    def keep_copy(j):
+        spot = yr.at[place * chunks + j, pl.ds(pl.multiple_of(mp * part, part), part)]
+        return pltpu.make_async_copy(spot, result(mp * chunks + j), keep_sem.at[j])
 
     def part_copy(o):
         other = lax.rem(me + o, devices)
         return pltpu.make_async_remote_copy(
-            parts.at[0], parts.at[devices - o], p_send, p_recv, device_id=(other // owners, other % owners), device_id_type=MESH
-        )
-
-    def out_copy(i):
-        return pltpu.make_async_copy(
-            g.at[i], g_hbm.at[:, pl.ds(pl.multiple_of(i * wide, wide), wide)], out_sem.at[i]
-        )
-
-    def produce(q, on, k, to_lane, j, fresh, parity):
+            parts.at[0, pl.ds(0, 1)], parts.at[devices - o, pl.ds(0, 1)], p_send, p_recv,
+            device_id=(other // owners, other % owners), device_id_type=MESH,
+        )
+
+    def produce(q, on, k, to_lane, j, fresh, first_use, parity, first_tick=None):
         @pl.when(on)
         def _():
+            @pl.when(first_use)
+            def _():
+                x_in(k, to_lane).wait()
+
             @pl.when(fresh)
             def _():
                 for side, owner in enumerate((1 - core, core)):
@@ -169,6 +196,12 @@
             cols = pl.ds(pl.multiple_of(j * wide, wide), wide)
             sb[q] = jnp.dot(xt[q, 0], c[:, cols], preferred_element_type=jnp.float32)
             ob[q] = jnp.dot(xt[q, 1], c[:, cols], preferred_element_type=jnp.float32)
+
+            if q == 0:
+                @pl.when(first_tick)
+                def _():
+                    pl.semaphore_wait(barrier, devices - 1)
+
             core_copy(q, parity).start()
 
     def own(q, on, k, j, parity):
@@ -186,6 +219,7 @@
 
             @pl.when(jnp.logical_not(crossed))
             def _():
+                d_copy(j).wait_send()
                 yr[idx] = ob[q] + rb[parity, q]
 
             @pl.when((k >= place) & (place > 0))
@@ -211,7 +245,7 @@
                     x_copy(o, j).start()
                 value = yr[idx]
                 sq[...] += jnp.sum((value * value).reshape(rows // 8, 8, wide), axis=0)
-                g[mp * chunks + j] = yr[idx, pl.ds(pl.multiple_of(mp * part, part), part)]
+                keep_copy(j).start()
 
     @pl.loop(0, plan.ticks)
     def _(t):
@@ -236,10 +270,21 @@
         s_k = mirrored(jnp.where(backward, n // chunks, at))
         s_j = jnp.where(backward, n % chunks, t - plan.last)
 
-        produce(0, crossing, y_k, 1 - lane, y_j, step == 0, parity)
-        produce(1, deferring, beside, 1 - lane, t, t == 0, parity)
-        produce(2, m_on, m_k, lane, m_j, m_j == 0, parity)
-        produce(3, s_on, s_k, lane, s_j, s_j == 0, parity)
+        @pl.when(t < chunks)
+        def _():
+            ready(t)
+
+        third_k = jnp.where(deferring, beside, s_k)
+        third_j = jnp.where(deferring, t, s_j)
+        third_lane = jnp.where(deferring, 1 - lane, lane)
+        produce(0, crossing, y_k, 1 - lane, y_j, step == 0, (y_j == 0) & (y_k != beside), parity, t == 0)
+
+        @pl.when(t == 0)
+        def _():
+            load_rest()
+
+        produce(1, m_on, m_k, lane, m_j, m_j == 0, m_j == 0, parity)
+        produce(2, deferring | s_on, third_k, third_lane, third_j, third_j == 0, third_j == 0, parity)
 
         slot = lax.rem(t, RING)
         y_idx = y_k * chunks + y_j
@@ -262,49 +307,22 @@
 
         @pl.when(deferring)
         def _():
-            core_copy(1, parity).wait()
-            ds[t] = ob[1] + rb[parity, 1]
+            core_copy(2, parity).wait()
+            yr[beside * chunks + t] = ob[2] + rb[parity, 2]
             d_copy(t).start()
 
-        own(2, m_on, m_k, m_j, parity)
-        own(3, s_on, s_k, s_j, parity)
+        own(1, m_on, m_k, m_j, parity)
+        own(2, s_on, s_k, s_j, parity)
 
     total = sq[:, pl.ds(0, 128)]
     for i in range(1, wide // 128):
         total = total + sq[:, pl.ds(i * 128, 128)]
-    parts[0] = total
+    parts[0, pl.ds(0, 1)] = jnp.sum(total, axis=0, keepdims=True)
 
     @pl.loop(1, devices)
     def _(o):
         part_copy(o).start()
 
-    @pl.loop(0, chunks)
-    def _(j):
-        out_copy(mp * chunks + j).start()
-
-    for o in range(1, owners):
-        @pl.loop(0, chunks)
-        def _(j):
-            i = lax.rem(mp + o, owners) * chunks + j
-            pltpu.make_async_remote_copy(
-                g.at[i], g.at[i], x_send.at[0], x_recv.at[i], device_id=(dp, mp), device_id_type=MESH
-            ).wait_recv()
-            out_copy(i).start()
-
-    others = parts.at[pl.ds(1, devices - 1)]
-    everyone = pltpu.make_async_remote_copy(others, others, p_send, p_recv, device_id=(dp, mp), device_id_type=MESH)
-    everyone.wait_recv()
-    total_ref[...] = jnp.full(total_ref.shape, jnp.sum(jnp.sum(parts[...], axis=0)))
-    everyone.wait_send()
-
-    @pl.loop(0, owners * chunks)
-    def _(i):
-        out_copy(i).wait()
-
-    @pl.loop(0, half)
-    def _(j):
-        d_copy(j).wait_send()
-
     @pl.loop(0, RING)
     def _(slot):
         y_copy(slot, 0).wait_send()
@@ -314,14 +332,27 @@
         @pl.when(i // chunks != place)
         def _():
             z_copy(i, 0, place).wait_send()
+
+    @pl.loop(0, chunks)
+    def _(j):
+        keep_copy(j).wait()
 
     for o in range(1, owners):
         @pl.loop(0, chunks)
         def _(j):
             x_copy(o, j).wait_send()
-
-
-def reduced_gradient(plan, ff_blocks, layer_active, rows_in, rows_ct):
+            i = lax.rem(mp + o, owners) * chunks + j
+            pltpu.make_async_remote_copy(
+                result(i), result(i), x_send.at[0], x_recv.at[i], device_id=(dp, mp), device_id_type=MESH
+            ).wait_recv()
+
+    everyone = parts.at[pl.ds(1, devices - 1), pl.ds(0, 1)]
+    arrivals = pltpu.make_async_remote_copy(everyone, everyone, p_send, p_recv, device_id=(dp, mp), device_id_type=MESH)
+    arrivals.wait()
+    total_ref[0, 0] = jnp.sum(jnp.sum(parts[:, pl.ds(0, 1), :], axis=0))
+
+
+def reduced_gradient(plan, limit, rows_in, rows_ct):
     rows, wide, chunks, line, half = plan.rows, plan.wide, plan.chunks, plan.line, plan.half
     devices = plan.replicas * plan.owners
     f32, dma = jnp.float32, pltpu.SemaphoreType.DMA
@@ -329,37 +360,39 @@
     def held(*lead):
         return pltpu.VMEM((*lead, rows, wide), f32)
 
+    buffers = [
+        pltpu.VMEM((plan.tokens, plan.width), jnp.bfloat16),
+        pltpu.VMEM((plan.tokens, plan.cols), jnp.bfloat16),
+        pltpu.VMEM((3, 2, rows, plan.tokens), jnp.bfloat16),
+        held(RING),
+        held(line * chunks),
+        held((line + 1) * chunks),
+        held(half),
+        held(3),
+        held(2, 3),
+        held(3),
+        pltpu.VMEM((8, wide), f32),
+        pltpu.VMEM((devices, 8, 128), f32),
+    ]
+    room = sum(math.prod(b.shape) * jnp.dtype(b.dtype).itemsize for b in buffers)
     return pl.pallas_call(
         functools.partial(kernel, plan),
         out_shape=(
             jax.ShapeDtypeStruct((plan.part, plan.owners * plan.cols), f32),
-            jax.ShapeDtypeStruct((8, 128), f32),
+            jax.ShapeDtypeStruct((1, 1), f32),
         ),
         in_specs=[
-            pl.BlockSpec(memory_space=pltpu.SMEM),
             pl.BlockSpec(memory_space=pltpu.SMEM),
             pl.BlockSpec(memory_space=pl.ANY),
             pl.BlockSpec(memory_space=pl.ANY),
         ],
-        out_specs=(pl.BlockSpec(memory_space=pl.ANY), pl.BlockSpec(memory_space=pltpu.VMEM)),
+        out_specs=(pl.BlockSpec(memory_space=pl.ANY), pl.BlockSpec(memory_space=pltpu.SMEM)),
         scratch_shapes=[
-            pltpu.VMEM((plan.tokens, plan.width), jnp.bfloat16),
-            pltpu.VMEM((plan.tokens, plan.cols), jnp.bfloat16),
-            pltpu.VMEM((4, 2, rows, plan.tokens), jnp.bfloat16),
-            held(RING),
-            held(line * chunks),
-            held((line + 1) * chunks),
-            held(half),
-            held(half),
-            held(4),
-            held(2, 4),
-            held(4),
-            pltpu.VMEM((plan.owners * chunks, plan.part, wide), f32),
-            pltpu.VMEM((8, wide), f32),
-            pltpu.VMEM((devices, 8, 128), f32),
-            dma((2,)),
-            dma((4,)),
-            dma((2, 4)),
+            *buffers,
+            dma((line * 2,)),
+            dma((chunks,)),
+            dma((3,)),
+            dma((2, 3)),
             dma((RING,)),
             dma((line * chunks,)),
             dma((line * chunks,)),
@@ -368,16 +401,16 @@
             dma((half,)),
             dma((max(1, plan.owners - 1) * chunks,)),
             dma((plan.owners * chunks,)),
-            dma((plan.owners * chunks,)),
+            dma((chunks,)),
             dma,
             dma,
         ],
-        compiler_params=pltpu.CompilerParams(collective_id=0, has_side_effects=True, vmem_limit_bytes=67043328),
+        compiler_params=pltpu.CompilerParams(collective_id=0, has_side_effects=True, vmem_limit_bytes=room + (1 << 20)),
         cost_estimate=pl.CostEstimate(
             flops=2 * plan.tokens * plan.width * plan.cols, bytes_accessed=32 << 20, transcendentals=0
         ),
         name="reduced_gradient",
-    )(ff_blocks, layer_active, rows_in, rows_ct)
+    )(limit, rows_in, rows_ct)
 
 
 def shards(inputs, gate_cotangent, ff_blocks, layer_active, param, moment, second_moment):
@@ -387,8 +420,7 @@
     plan = Plan(replicas, owners, width, local_cols, subnets * tokens)
     gradient, total_sq = reduced_gradient(
         plan,
-        ff_blocks,
-        layer_active,
+        jnp.where(layer_active == 1, ff_blocks, 0),
         inputs.reshape(subnets * tokens, width),
         gate_cotangent.reshape(subnets * tokens, local_cols),
     )

time: 271 us -> 261 us (0.963)
  Pallas kernels: 259 us -> 255 us
  other arithmetic: 8.31 us -> 5.18 us
    pallas_call x1, Pallas kernels: 259 us -> 255 us  [reduced_gradient(): pl.pallas_call(functools.partial(kernel, plan), out_shape=(jax.ShapeDtype...]
    sub x1, other arithmetic: 8.31 us -> 4.51 us  [shards(): param - 0.02 * (first_hat / (jnp.sqrt(second_hat) + 1e-08) + 0.1 * param)]
where the time goes in v1:
time: 261 us
  Pallas kernels  255 us (98%)
  other arithmetic  5.18 us (2%)
    pallas_call x1, Pallas kernels, reduced_gradient(): pl.pallas_call(functools.partial(kernel, plan), out_shape=(jax.ShapeDtype...  255 us

profile of v1, /device:TPU:0, one launch (start us, length us, event | category | flops | bytes accessed | tf_op | source)
XLA Modules:
  0.0 261.3 jit_solution(4028584516572111359)
XLA Ops:
  0.6 0.7 compare_select_fusion.limit
  1.3 0.0 copy-start
  1.3 0.0 copy-start.1
  1.3 0.0 copy-start.2
  1.3 254.7 %reduced_gradient.1 = (f32[128,6144]{1,0:T(8,128)S(1)}, f32[1,1]{1,0:T(1,128)}) custom-call(s32[4]{0:T(128)S(1)} %compare_select_fusion.limit, bf16[1024,4096]{1,0:T(8,128)(2,1)} %bitcast.3, bf16[1024,3072]{1,0:T(8,128)(2,1)} %bitcast.4), custom_call_target="tpu_custom_call" | custom-call | flops 25769803776 | bytes 33554432 | tf_op jit(solution)/shard_map/reduced_gradient/pallas_call | solution.py:378
  256.7 0.0 copy-done
  256.7 0.0 copy-done.1
  256.7 0.0 copy-done.2
  256.7 4.5 %multiply_subtract_fusion = (f32[128,6144]{1,0:T(8,128)}, f32[128,6144]{1,0:T(8,128)}, f32[128,6144]{1,0:T(8,128)}) fusion(f32[128,6144]{1,0:T(8,128)S(1)} %copy-done, f32[128,6144]{1,0:T(8,128)S(1)} %get-tuple-element.5, f32[]{:T(128)} %bitcast.2, f32[128,6144]{1,0:T(8,128)S(1)} %copy-done.1, f32[128,6144]{1,0:T(8,128)S(1)} %copy-done.2), kind=kLoop, calls=%fused_computation.2 | loop fusion | flops 12582912 | bytes 22020100 | tf_op jit(solution)/shard_map/sub | solution.py:434
Async XLA Ops:
  1.3 255.4 %copy-start = (f32[128,6144]{1,0:T(8,128)S(1)}, f32[128,6144]{1,0:T(8,128)}, u32[]{:S(2)}) copy-start(f32[128,6144]{1,0:T(8,128)} %param.11) | copy-start | bytes 9437188
  1.3 255.4 %copy-start.1 = (f32[128,6144]{1,0:T(8,128)S(1)}, f32[128,6144]{1,0:T(8,128)}, u32[]{:S(2)}) copy-start(f32[128,6144]{1,0:T(8,128)} %param.12) | copy-start | bytes 9437188
  1.3 255.4 %copy-start.2 = (f32[128,6144]{1,0:T(8,128)S(1)}, f32[128,6144]{1,0:T(8,128)}, u32[]{:S(2)}) copy-start(f32[128,6144]{1,0:T(8,128)} %param.13) | copy-start | bytes 9437188

commit v2 on v1

--- a/solution.py
+++ b/solution.py
@@ -74,7 +74,7 @@
 
 def kernel(plan, limit, x_hbm, c_hbm, g_hbm, total_ref, x, c, xt, w, yr, z, dr, sb, rb, ob, sq, parts,
            x_load, c_load, d2d_send, d2d_recv, y_send, y_recv, z_send, z_recv, d_send, d_recv, x_send, x_recv, keep_sem,
-           p_send, p_recv):
+           p_send, p_recv, y_tail, z_tail):
     line, chunks, half, rows, wide = plan.line, plan.chunks, plan.half, plan.rows, plan.wide
     owners, part = plan.owners, plan.part
     dp, mp = lax.axis_index("dp"), lax.axis_index("mp")
@@ -158,6 +158,25 @@
             yr.at[idx], z.at[slot], z_send.at[idx], z_recv.at[slot], device_id=(dp + 4 * (to - place), mp), device_id_type=MESH
         )
 
+    turns = [*range(1, owners), 0]
+
+    def piece(o):
+        return pl.ds(pl.multiple_of(lax.rem(mp + o, owners) * part, part), part)
+
+    def y_piece(slot, idx, o):
+        arrived = y_tail.at[(idx // chunks) * (owners - 1) + o - 1] if o else y_recv.at[idx]
+        return pltpu.make_async_remote_copy(
+            w.at[slot, piece(o)], yr.at[idx, piece(o)], y_send.at[slot], arrived,
+            device_id=(other_lane, mp), device_id_type=MESH,
+        )
+
+    def z_piece(idx, slot, to, o):
+        arrived = z_tail.at[(slot // chunks) * (owners - 1) + o - 1] if o else z_recv.at[slot]
+        return pltpu.make_async_remote_copy(
+            yr.at[idx, piece(o)], z.at[slot, piece(o)], z_send.at[idx], arrived,
+            device_id=(dp + 4 * (to - place), mp), device_id_type=MESH,
+        )
+
     def result(i):
         return g_hbm.at[:, pl.ds(pl.multiple_of(i * wide, wide), wide)]
 
@@ -204,12 +223,18 @@
 
             core_copy(q, parity).start()
 
+    def squares(value):
+        sq[...] += jnp.sum((value * value).reshape(value.shape[0] // 8, 8, wide), axis=0)
+
     def own(q, on, k, j, parity):
         idx = k * chunks + j
-
-        @pl.when(on)
-        def _():
-            core_copy(q, parity).wait()
+        from_left = (k >= place) & (place > 0)
+        from_right = (k <= place) & (place < line - 1)
+        right_slot = jnp.where(k == place, line, k) * chunks + j
+        to = jnp.where(k > place, place + 1, place - 1)
+        to_slot = jnp.where(k == place - 1, line, k) * chunks + j
+
+        def whole():
             crossed = (k != beside) | (j >= half)
 
             @pl.when(crossed)
@@ -222,30 +247,66 @@
                 d_copy(j).wait_send()
                 yr[idx] = ob[q] + rb[parity, q]
 
-            @pl.when((k >= place) & (place > 0))
+            @pl.when(from_left)
             def _():
                 z_copy(idx, idx, place).wait_recv()
                 yr[idx] = yr[idx] + z[idx]
 
-            @pl.when((k <= place) & (place < line - 1))
-            def _():
-                slot = jnp.where(k == place, line, k) * chunks + j
-                z_copy(idx, slot, place).wait_recv()
-                yr[idx] = yr[idx] + z[slot]
+            @pl.when(from_right)
+            def _():
+                z_copy(idx, right_slot, place).wait_recv()
+                yr[idx] = yr[idx] + z[right_slot]
 
             @pl.when(k != place)
             def _():
-                to = jnp.where(k > place, place + 1, place - 1)
-                slot = jnp.where(k == place - 1, line, k) * chunks + j
-                z_copy(idx, slot, to).start()
+                z_copy(idx, to_slot, to).start()
 
             @pl.when(k == place)
             def _():
                 for o in range(1, owners):
                     x_copy(o, j).start()
-                value = yr[idx]
-                sq[...] += jnp.sum((value * value).reshape(rows // 8, 8, wide), axis=0)
+                squares(yr[idx])
                 keep_copy(j).start()
+
+        def in_pieces(o):
+            spot = piece(o)
+            y_piece(0, idx, o).wait_recv()
+            yr[idx, spot] = yr[idx, spot] + (ob[q, spot] + rb[parity, q, spot])
+
+            @pl.when(from_left)
+            def _():
+                z_piece(idx, idx, place, o).wait_recv()
+                yr[idx, spot] = yr[idx, spot] + z[idx, spot]
+
+            @pl.when(from_right)
+            def _():
+                z_piece(idx, right_slot, place, o).wait_recv()
+                yr[idx, spot] = yr[idx, spot] + z[right_slot, spot]
+
+            @pl.when(k != place)
+            def _():
+                z_piece(idx, to_slot, to, o).start()
+
+            @pl.when(k == place)
+            def _():
+                if o:
+                    x_copy(o, j).start()
+                squares(yr[idx, spot])
+                if not o:
+                    keep_copy(j).start()
+
+        @pl.when(on)
+        def _():
+            core_copy(q, parity).wait()
+
+            @pl.when(j < chunks - 1)
+            def _():
+                whole()
+
+            @pl.when(j == chunks - 1)
+            def _():
+                for o in turns:
+                    in_pieces(o)
 
     @pl.loop(0, plan.ticks)
     def _(t):
@@ -303,7 +364,14 @@
                 d_copy(y_j).wait_recv()
                 w[slot] = w[slot] + dr[y_j]
 
-            y_copy(slot, y_idx).start()
+            @pl.when(y_j < chunks - 1)
+            def _():
+                y_copy(slot, y_idx).start()
+
+            @pl.when(y_j == chunks - 1)
+            def _():
+                for o in turns:
+                    y_piece(slot, y_idx, o).start()
 
         @pl.when(deferring)
         def _():
@@ -404,6 +472,8 @@
             dma((chunks,)),
             dma,
             dma,
+            dma((line * max(1, plan.owners - 1),)),
+            dma(((line + 1) * max(1, plan.owners - 1),)),
         ],
         compiler_params=pltpu.CompilerParams(collective_id=0, has_side_effects=True, vmem_limit_bytes=room + (1 << 20)),
         cost_estimate=pl.CostEstimate(

time: 261 us -> 261 us (level)
  no operation moved by 1% of the time
where the time goes in v2:
time: 261 us
  Pallas kernels  255 us (98%)
  other arithmetic  5.18 us (2%)
    pallas_call x1, Pallas kernels, reduced_gradient(): pl.pallas_call(functools.partial(kernel, plan), out_shape=(jax.ShapeDtype...  255 us

profile of v2, /device:TPU:0, one launch (start us, length us, event | category | flops | bytes accessed | tf_op | source)
XLA Modules:
  0.0 261.3 jit_solution(5256814211387054157)
XLA Ops:
  0.6 0.7 compare_select_fusion.limit
  1.3 0.0 copy-start
  1.3 0.0 copy-start.1
  1.3 0.0 copy-start.2
  1.3 254.7 %reduced_gradient.1 = (f32[128,6144]{1,0:T(8,128)S(1)}, f32[1,1]{1,0:T(1,128)}) custom-call(s32[4]{0:T(128)S(1)} %compare_select_fusion.limit, bf16[1024,4096]{1,0:T(8,128)(2,1)} %bitcast.3, bf16[1024,3072]{1,0:T(8,128)(2,1)} %bitcast.4), custom_call_target="tpu_custom_call" | custom-call | flops 25769803776 | bytes 33554432 | tf_op jit(solution)/shard_map/reduced_gradient/pallas_call | solution.py:446
  256.7 0.0 copy-done
  256.8 0.0 copy-done.1
  256.8 0.0 copy-done.2
  256.8 4.5 %multiply_subtract_fusion = (f32[128,6144]{1,0:T(8,128)}, f32[128,6144]{1,0:T(8,128)}, f32[128,6144]{1,0:T(8,128)}) fusion(f32[128,6144]{1,0:T(8,128)S(1)} %copy-done, f32[128,6144]{1,0:T(8,128)S(1)} %get-tuple-element.5, f32[]{:T(128)} %bitcast.2, f32[128,6144]{1,0:T(8,128)S(1)} %copy-done.1, f32[128,6144]{1,0:T(8,128)S(1)} %copy-done.2), kind=kLoop, calls=%fused_computation.2 | loop fusion | flops 12582912 | bytes 22020100 | tf_op jit(solution)/shard_map/sub | solution.py:504
Async XLA Ops:
  1.3 255.4 %copy-start = (f32[128,6144]{1,0:T(8,128)S(1)}, f32[128,6144]{1,0:T(8,128)}, u32[]{:S(2)}) copy-start(f32[128,6144]{1,0:T(8,128)} %param.11) | copy-start | bytes 9437188
  1.3 255.4 %copy-start.1 = (f32[128,6144]{1,0:T(8,128)S(1)}, f32[128,6144]{1,0:T(8,128)}, u32[]{:S(2)}) copy-start(f32[128,6144]{1,0:T(8,128)} %param.12) | copy-start | bytes 9437188
  1.3 255.5 %copy-start.2 = (f32[128,6144]{1,0:T(8,128)S(1)}, f32[128,6144]{1,0:T(8,128)}, u32[]{:S(2)}) copy-start(f32[128,6144]{1,0:T(8,128)} %param.13) | copy-start | bytes 9437188
